TPU v7x, 512 devices: a whole 4x4x16 slice. The times are simulated.
512 devices in a mesh: seq: 64 (over z_hi, x, y), chan: 8 (over z_lo, core).
Axes of the slice: x: 4, y: 4, z: 16 (z_hi: 4, z_lo: 4; z = z_hi * 4 + z_lo), core: 2. Of those that a mesh axis runs over, the one named last changes fastest.
Arguments:
- query_gate: bfloat16 [4096, 8192], P('chan', 'seq'), may hold values from -6 to 6
- key_gate: bfloat16 [4096, 8192], P('chan', 'seq'), may hold values from -6 to 6
- value_in: bfloat16 [4096, 8192], P('chan', 'seq'), may hold values from -6 to 6
- cotangent: bfloat16 [4096, 8192], P('chan', 'seq'), may hold values from -6 to 6
- long_filter: float32 [4096, 8192], P(('chan', 'seq')), may hold values from -0.0625 to 0.0625
- short_taps: float32 [4096, 3], P('chan'), may hold values from -3 to 3
Outputs:
- query_grad: bfloat16 [4096, 8192], P('chan', 'seq')
- key_grad: bfloat16 [4096, 8192], P('chan', 'seq')
- value_grad: bfloat16 [4096, 8192], P('chan', 'seq')
- filter_grad: float32 [4096, 8192], P(('chan', 'seq'))
- taps_grad: float32 [4096, 3], P('chan')
All inputs are finite; a program needn't handle non-finite values.
Results may differ from a plain program's by a relative error of at most 0.0064.
Values may be sent and summed in bfloat16 or wider, within the bound.
A program may use at most 64 MiB of HBM per device.

v0:
```python
import math

import jax
import jax.numpy as jnp
import ml_dtypes
import numpy as np
from jax import lax
from jax.experimental import pallas as pl
from jax.experimental.pallas import tpu as pltpu
from jax.sharding import PartitionSpec as P

TAPS = 3
MESH = pl.DeviceIdType.MESH
BF = jnp.bfloat16
F32 = jnp.float32

S = 64
W = 128
C = 8
N = S * W
PLANE = 16
HI = 4


def halves(table):
    hi = table.astype(ml_dtypes.bfloat16)
    lo = (table - hi.astype(np.float64)).astype(ml_dtypes.bfloat16)
    return hi, lo


def tables():
    quarter = np.arange(S) + 0.25
    rows = 2.0 * np.pi * np.outer(quarter, np.arange(S)) / S
    twist = 2.0 * np.pi * np.outer(quarter, np.arange(W)) / N
    cols = 2.0 * np.pi * np.outer(np.arange(W), np.arange(W)) / W
    a_hi, a_lo = halves(np.concatenate([np.cos(rows), -np.sin(rows)], axis=0))
    b_hi, b_lo = halves(np.concatenate([np.cos(rows).T, -np.sin(rows).T], axis=1) / N)
    fr, fi = np.cos(cols), -np.sin(cols)
    f_hi, f_lo = halves(np.block([[fr, fi], [-fi, fr]]))
    g_hi, g_lo = halves(np.block([[fr, -fi], [fi, fr]]))
    first = np.concatenate([a_hi, a_lo, a_hi, a_lo], axis=1)
    last = np.concatenate([b_hi, b_lo, b_hi], axis=1)
    middle = np.stack([f_hi, f_lo, g_hi, g_lo])
    turn = np.stack([np.cos(twist), -np.sin(twist)]).astype(np.float32)
    return first, middle, last, turn


def split(x):
    hi = x.astype(BF)
    return hi, (x - hi.astype(F32)).astype(BF)


def dot(a, b):
    return jnp.dot(a, b, preferred_element_type=F32)


def wide(table):
    return jnp.concatenate([table] * C, axis=1)


def to_rows(x):
    return jnp.concatenate([x[:, c * W : (c + 1) * W] for c in range(C)], axis=0)


def to_cols(x):
    return jnp.concatenate([x[c * S : (c + 1) * S] for c in range(C)], axis=1)


def forward(stacked, first, middle, turn):
    y = dot(first, stacked)
    yr, yi = y[:S], y[S:]
    tc, ts = wide(turn[0]), wide(turn[1])
    turned = jnp.concatenate([to_rows(yr * tc - yi * ts), to_rows(yr * ts + yi * tc)], axis=1)
    hi, lo = split(turned)
    return dot(hi, middle[0]) + dot(lo, middle[0]) + dot(hi, middle[1])


def inverse(spec_re, spec_im, middle, last, turn):
    hi, lo = split(jnp.concatenate([spec_re, spec_im], axis=1))
    v = dot(hi, middle[2]) + dot(lo, middle[2]) + dot(hi, middle[3])
    vr, vi = to_cols(v[:, :W]), to_cols(v[:, W:])
    tc, ts = wide(turn[0]), wide(turn[1])
    hi, lo = split(jnp.concatenate([vr * tc + vi * ts, vi * tc - vr * ts], axis=0))
    return dot(last[...], jnp.concatenate([hi, hi, lo], axis=0))


def load_signal(ref):
    return jnp.concatenate([ref[pl.ds(c, S, stride=C), :] for c in range(C)], axis=1)


def store_signal(ref, x):
    for c in range(C):
        ref[pl.ds(c, S, stride=C), :] = x[:, c * W : (c + 1) * W]


def row_pick(rows, lanes):
    r = lax.broadcasted_iota(jnp.int32, (8, W), 0)
    l = lax.broadcasted_iota(jnp.int32, (8, W), 1)
    hit = None
    for row, lane in zip(rows, lanes):
        one = (r == row) & (l == lane)
        hit = one if hit is None else hit | one
    return hit.astype(F32)


def pack_pair(x, lanes):
    total = None
    for b in range(4):
        part = lax.dot_general(
            row_pick((2 * b, 2 * b + 1), lanes).astype(BF),
            x[b * W : (b + 1) * W],
            (((1,), (1,)), ((), ())),
            preferred_element_type=F32,
        )
        total = part if total is None else total + part
    return total


def unpack_pair(packed, lanes):
    turned = packed.T.astype(BF)
    return jnp.concatenate(
        [dot(turned, row_pick((2 * b, 2 * b + 1), lanes).astype(BF)) for b in range(4)], axis=0
    )


def main_kernel(
    q_ref, k_ref, v_ref, cot_ref, h_ref, a_ref, first_ref, mid_ref, last_ref, turn_ref,
    qg_ref, kg_ref, vg_ref, fg_ref, tg_ref,
    g_out, g_in, m_out, m_in, b_out, b_in, c_out, c_in,
    vh_out, vh_in, fh_out, fh_in, tp_out, tp_in, tz_out, tz_in,
    rows_ref, filt_ref, low_ref, hs_ref, gs_ref, ms_ref,
    send_sems, recv_sems,
):
    me = lax.axis_index("seq")
    after, before = lax.rem(me + 1, S), lax.rem(me + S - 1, S)
    barrier = pltpu.get_barrier_semaphore()

    def greet(i, carry):
        pl.semaphore_signal(
            barrier, inc=1, device_id={"seq": lax.rem(me + i, S)}, device_id_type=MESH
        )
        return carry

    lax.fori_loop(1, S, greet, 0)

    def remote(src, dst, index, to):
        return pltpu.make_async_remote_copy(
            src_ref=src, dst_ref=dst, send_sem=send_sems.at[index], recv_sem=recv_sems.at[index],
            device_id={"seq": to}, device_id_type=MESH,
        )

    def exchange(out, into, index):
        def one(i, carry):
            to = lax.rem(me + i, S)
            remote(out.at[to], into.at[me], index, to).start()
            return carry

        lax.fori_loop(1, S, one, 0)
        into[me] = out[me]

    def arrived(buffer, sem, count):
        part = buffer.at[pl.ds(0, count)]
        pltpu.make_async_copy(part, part, sem).wait()

    first, turn = first_ref, turn_ref

    cot = cot_ref[...].astype(F32)
    g_out[...] = (cot * q_ref[...].astype(F32)).astype(BF).reshape(S, C, W)
    vh_out[...] = pack_pair(v_ref[...], (W - 2, W - 1))
    for n in range(S):
        rows_ref[n * C : (n + 1) * C, :] = h_ref[:, n * W : (n + 1) * W]
    hi, lo = split(load_signal(rows_ref))
    hs_ref[...] = forward(jnp.concatenate([hi, hi, lo, lo], axis=0), first[...], mid_ref, turn)

    pl.semaphore_wait(barrier, S - 1)

    halo_v = remote(vh_out, vh_in, 0, after)
    halo_v.start()
    exchange(g_out, g_in, 1)

    value = v_ref[...].astype(F32)
    halo_v.wait()
    held = jnp.where(me > 0, vh_in[...], 0.0)
    value_prev = unpack_pair(held, (W - 2, W - 1))
    lane = lax.broadcasted_iota(jnp.int32, (C * S, W), 1)

    def lagged(j):
        if j == 0:
            return value
        return jnp.where(lane < j, pltpu.roll(value_prev, j, 1), pltpu.roll(value, j, 1))

    filtered = a_ref[:, 0:1] * value
    for j in range(1, TAPS):
        filtered = filtered + a_ref[:, j : j + 1] * lagged(j)
    filt_ref[...] = filtered
    m_out[...] = (k_ref[...].astype(F32) * filtered).astype(BF).reshape(S, C, W)
    exchange(m_out, m_in, 2)

    def take(buffer):
        rows_ref[...] = buffer[...].astype(F32).reshape(S * C, W)
        x = load_signal(rows_ref).astype(BF)
        return forward(jnp.concatenate([x, x], axis=0), first[:, : 2 * S], mid_ref, turn)

    def give(buffer, x):
        store_signal(rows_ref, x)
        buffer[...] = rows_ref[...].astype(BF).reshape(S, C, W)

    arrived(g_in, recv_sems.at[1], S - 1)
    grad = take(g_in)
    gs_ref[...] = grad
    hs = hs_ref[...]
    hr, hi_ = hs[:, :W], hs[:, W:]
    gr, gi = grad[:, :W], grad[:, W:]
    give(b_out, inverse(hr * gr + hi_ * gi, hr * gi - hi_ * gr, mid_ref, last_ref, turn))
    exchange(b_out, b_in, 3)

    arrived(m_in, recv_sems.at[2], S - 1)
    mixed = take(m_in)
    ms_ref[...] = mixed
    hs = hs_ref[...]
    hr, hi_ = hs[:, :W], hs[:, W:]
    mr, mi = mixed[:, :W], mixed[:, W:]
    give(c_out, inverse(mr * hr - mi * hi_, mr * hi_ + mi * hr, mid_ref, last_ref, turn))
    exchange(c_out, c_in, 4)

    mixed, grad = ms_ref[...], gs_ref[...]
    mr, mi = mixed[:, :W], mixed[:, W:]
    gr, gi = grad[:, :W], grad[:, W:]
    fg = inverse(mr * gr + mi * gi, mr * gi - mi * gr, mid_ref, last_ref, turn)
    store_signal(rows_ref, fg * (1.0 / math.sqrt(N)))
    for n in range(S):
        fg_ref[:, n * W : (n + 1) * W] = rows_ref[n * C : (n + 1) * C, :]

    arrived(b_in, recv_sems.at[3], S - 1)
    back = b_in[...].astype(F32).reshape(S * C, W)
    kg_ref[...] = (back * filt_ref[...]).astype(BF)
    low_bf = (back * k_ref[...].astype(F32)).astype(BF)
    low_ref[...] = low_bf.astype(F32)
    fh_out[...] = pack_pair(low_bf, (0, 1))
    halo_f = remote(fh_out, fh_in, 5, before)
    halo_f.start()

    low = low_ref[...]
    row8 = lax.broadcasted_iota(jnp.int32, (8, W), 0)
    partial = jnp.zeros((8, 2 * W), F32)
    for j in range(TAPS):
        terms = low * lagged(j)
        t1, rest = split(terms)
        t1f = t1.astype(F32)
        t2, t3 = split(terms - t1f)
        for half in range(2):
            mark = (row8 == 4 * half + j).astype(BF)
            for piece in (t1, t2, t3):
                partial = partial + lax.dot_general(
                    mark, piece[half * 2 * W : (half + 1) * 2 * W], (((1,), (1,)), ((), ())),
                    preferred_element_type=F32,
                )
    tp_out[...] = partial
    place, height = lax.rem(me, PLANE), me // PLANE

    def to_plane(i, carry):
        to = height * PLANE + lax.rem(place + i, PLANE)
        remote(tp_out, tp_in.at[place], 6, to).start()
        return carry

    lax.fori_loop(1, PLANE, to_plane, 0)
    tp_in[place] = tp_out[...]

    halo_f.wait()
    held = jnp.where(me < S - 1, fh_in[...], 0.0)
    low_next = unpack_pair(held, (0, 1))
    value_grad = a_ref[:, 0:1] * low
    for j in range(1, TAPS):
        ahead = jnp.where(lane >= W - j, pltpu.roll(low_next, W - j, 1), pltpu.roll(low, W - j, 1))
        value_grad = value_grad + a_ref[:, j : j + 1] * ahead
    vg_ref[...] = value_grad.astype(BF)

    arrived(tp_in, recv_sems.at[6], PLANE - 1)
    tz_out[...] = jnp.sum(tp_in[...], axis=0)

    def to_heights(i, carry):
        to = lax.rem(height + i, HI) * PLANE + place
        remote(tz_out, tz_in.at[height], 7, to).start()
        return carry

    lax.fori_loop(1, HI, to_heights, 0)
    tz_in[height] = tz_out[...]

    arrived(c_in, recv_sems.at[4], S - 1)
    conv = c_in[...].astype(F32).reshape(S * C, W)
    qg_ref[...] = (cot_ref[...].astype(F32) * conv).astype(BF)

    arrived(tz_in, recv_sems.at[7], HI - 1)
    tg_ref[...] = jnp.sum(tz_in[...], axis=0) * (1.0 / math.sqrt(N))

    arrived(g_out, send_sems.at[1], S - 1)
    arrived(m_out, send_sems.at[2], S - 1)
    arrived(b_out, send_sems.at[3], S - 1)
    arrived(c_out, send_sems.at[4], S - 1)
    arrived(tp_in, send_sems.at[6], PLANE - 1)
    arrived(tz_in, send_sems.at[7], HI - 1)


def write_kernel(q_in, k_in, v_in, f_in, t_in, q_out, k_out, v_out, f_out, t_out):
    q_out[...] = q_in[...]
    k_out[...] = k_in[...]
    v_out[...] = v_in[...]
    f_out[...] = f_in[...]
    turned = t_in[...].T
    t_out[: 2 * W, :] = turned[:, :TAPS]
    t_out[2 * W :, :] = turned[:, 4 : 4 + TAPS]


def on_device(query_gate, key_gate, value_in, cotangent, long_filter, short_taps):
    rows, width = key_gate.shape
    first, middle, last, turn = (jnp.asarray(t) for t in tables())
    vmem = pl.BlockSpec(memory_space=pltpu.VMEM)
    stream = jax.ShapeDtypeStruct((rows, width), BF)
    filt = jax.ShapeDtypeStruct((C, N), F32)
    outs = pl.pallas_call(
        main_kernel,
        out_shape=(stream, stream, stream, filt, jax.ShapeDtypeStruct((8, 2 * W), F32)),
        in_specs=[vmem] * 10,
        out_specs=(vmem,) * 5,
        scratch_shapes=[pltpu.VMEM((S, C, W), BF)] * 8
        + [pltpu.VMEM((8, W), F32)] * 4
        + [
            pltpu.VMEM((8, 2 * W), F32),
            pltpu.VMEM((PLANE, 8, 2 * W), F32),
            pltpu.VMEM((8, 2 * W), F32),
            pltpu.VMEM((HI, 8, 2 * W), F32),
            pltpu.VMEM((S * C, W), F32),
            pltpu.VMEM((S * C, W), F32),
            pltpu.VMEM((S * C, W), F32),
            pltpu.VMEM((S * C, 2 * W), F32),
            pltpu.VMEM((S * C, 2 * W), F32),
            pltpu.VMEM((S * C, 2 * W), F32),
            pltpu.SemaphoreType.DMA((8,)),
            pltpu.SemaphoreType.DMA((8,)),
        ],
        compiler_params=pltpu.CompilerParams(
            collective_id=0, has_side_effects=True, vmem_limit_bytes=48 << 20
        ),
        name="exchange",
    )(query_gate, key_gate, value_in, cotangent, long_filter, short_taps, first, middle, last, turn)
    return pl.pallas_call(
        write_kernel,
        out_shape=(stream, stream, stream, filt, jax.ShapeDtypeStruct((rows, TAPS), F32)),
        in_specs=[vmem] * 5,
        out_specs=(vmem,) * 5,
        name="write",
    )(*outs)


def solution(mesh):
    spec = P("chan", "seq")
    owned = P(("chan", "seq"), None)
    taps = P("chan", None)
    return jax.shard_map(
        on_device,
        mesh=mesh,
        in_specs=(spec, spec, spec, spec, owned, taps),
        out_specs=(spec, spec, spec, owned, taps),
        check_vma=False,
    )
```

profile of v0, /device:TPU:64, one launch (start us, length us, event | category | flops | bytes accessed | tf_op | source)
XLA Modules:
  0.0 76.0 jit_solution(9153482108926319789)
XLA Ops:
  0.6 0.0 copy-start.1
  0.6 0.9 %copy.15.a_ref = f32[512,3]{1,0:T(8,128)S(1)} copy(f32[512,3]{0,1:T(4,128)} %param.15) | data formatting | bytes 12288 | tf_op args[5]
  1.5 0.1 copy-done.1
  1.6 0.0 copy-start
  1.6 1.0 %copy-done = bf16[4,256,256]{2,1,0:T(8,128)(2,1)S(1)} copy-done((bf16[4,256,256]{2,1,0:T(8,128)(2,1)S(1)}, bf16[4,256,256]{2,1,0:T(8,128)(2,1)}, u32[]{:S(2)}) %copy-start) | copy-done | bytes 524312
  2.6 0.0 copy-start.6
  2.6 0.9 %copy-done.6 = bf16[512,128]{1,0:T(8,128)(2,1)S(1)} copy-done((bf16[512,128]{1,0:T(8,128)(2,1)S(1)}, bf16[512,128]{1,0:T(8,128)(2,1)}, u32[]{:S(2)}) %copy-start.6) | copy-done | bytes 131096
  3.5 0.0 copy-start.7
  3.5 0.9 %copy-done.7 = bf16[512,128]{1,0:T(8,128)(2,1)S(1)} copy-done((bf16[512,128]{1,0:T(8,128)(2,1)S(1)}, bf16[512,128]{1,0:T(8,128)(2,1)}, u32[]{:S(2)}) %copy-start.7) | copy-done | bytes 131096
  4.5 0.0 copy-start.8
  4.5 0.9 %copy-done.8 = bf16[512,128]{1,0:T(8,128)(2,1)S(1)} copy-done((bf16[512,128]{1,0:T(8,128)(2,1)S(1)}, bf16[512,128]{1,0:T(8,128)(2,1)}, u32[]{:S(2)}) %copy-start.8) | copy-done | bytes 131096
  5.4 0.0 copy-start.9
  5.4 0.9 %copy-done.9 = bf16[512,128]{1,0:T(8,128)(2,1)S(1)} copy-done((bf16[512,128]{1,0:T(8,128)(2,1)S(1)}, bf16[512,128]{1,0:T(8,128)(2,1)}, u32[]{:S(2)}) %copy-start.9) | copy-done | bytes 131096
  6.3 0.0 copy-start.10
  6.3 0.8 %copy-done.10 = f32[2,64,128]{2,1,0:T(8,128)S(1)} copy-done((f32[2,64,128]{2,1,0:T(8,128)S(1)}, f32[2,64,128]{2,1,0:T(8,128)}, u32[]{:S(2)}) %copy-start.10) | copy-done | bytes 65560
  7.1 0.0 copy-start.11
  7.1 0.8 %copy-done.11 = bf16[128,256]{1,0:T(8,128)(2,1)S(1)} copy-done((bf16[128,256]{1,0:T(8,128)(2,1)S(1)}, bf16[128,256]{1,0:T(8,128)(2,1)}, u32[]{:S(2)}) %copy-start.11) | copy-done | bytes 65560
  7.9 0.0 copy-start.12
  7.9 0.8 %copy-done.12 = bf16[64,384]{1,0:T(8,128)(2,1)S(1)} copy-done((bf16[64,384]{1,0:T(8,128)(2,1)S(1)}, bf16[64,384]{1,0:T(8,128)(2,1)}, u32[]{:S(2)}) %copy-start.12) | copy-done | bytes 49176
  8.7 60.2 %exchange.1 = (bf16[512,128]{1,0:T(8,128)(2,1)S(1)}, bf16[512,128]{1,0:T(8,128)(2,1)S(1)}, bf16[512,128]{1,0:T(8,128)(2,1)S(1)}, f32[8,8192]{1,0:T(8,128)S(1)}, f32[8,256]{1,0:T(8,128)S(1)}) custom-call(bf16[512,128]{1,0:T(8,128)(2,1)S(1)} %copy-done.6, bf16[512,128]{1,0:T(8,128)(2,1)S(1)} %copy-done.7, bf16[512,128]{1,0:T(8,128)(2,1)S(1)} %copy-done.8, ...), custom_call_target="tpu_custom_call" | custom-call | tf_op jit(solution)/shard_map/exchange/pallas_call | solution.py:320
  68.9 0.0 copy-start.2
  68.9 0.7 copy-done.2
  69.6 0.0 copy-start.3
  69.6 0.6 copy-done.3
  70.2 0.0 copy-start.4
  70.2 0.7 copy-done.4
  70.9 0.0 copy-start.5
  70.9 0.6 copy-done.5
  71.6 0.0 copy-start.13
  71.6 0.6 copy-done.13
  72.2 2.2 %write.1 = (bf16[512,128]{1,0:T(8,128)(2,1)}, bf16[512,128]{1,0:T(8,128)(2,1)}, bf16[512,128]{1,0:T(8,128)(2,1)}, f32[8,8192]{1,0:T(8,128)}, f32[512,3]{1,0:T(8,128)}) custom-call(bf16[512,128]{1,0:T(8,128)(2,1)} %copy-done.3, bf16[512,128]{1,0:T(8,128)(2,1)} %copy-done.4, bf16[512,128]{1,0:T(8,128)(2,1)} %copy-done.5, f32[8,8192]{1,0:T(8,128)} %copy-done.2, ...), custom_call_target="tpu_custom_call" | custom-call | tf_op jit(solution)/shard_map/write/pallas_call | solution.py:346
  74.3 1.7 %copy.16 = f32[512,3]{0,1:T(4,128)} copy(f32[512,3]{1,0:T(8,128)} %get-tuple-element.19) | data formatting | bytes 12288 | tf_op jit(solution)/shard_map/write/pallas_call | solution.py:346
Async XLA Ops:
  0.6 1.0 %copy-start.1 = (f32[8,8192]{1,0:T(8,128)S(1)}, f32[8,8192]{1,0:T(8,128)}, u32[]{:S(2)}) copy-start(f32[8,8192]{1,0:T(8,128)} %h_ref.1) | copy-start | bytes 786436
  1.6 1.0 %copy-start = (bf16[4,256,256]{2,1,0:T(8,128)(2,1)S(1)}, bf16[4,256,256]{2,1,0:T(8,128)(2,1)}, u32[]{:S(2)}) copy-start(bf16[4,256,256]{2,1,0:T(8,128)(2,1)} %constant.9.clone.mid_ref) | copy-start | bytes 1572868
  2.6 0.9 %copy-start.6 = (bf16[512,128]{1,0:T(8,128)(2,1)S(1)}, bf16[512,128]{1,0:T(8,128)(2,1)}, u32[]{:S(2)}) copy-start(bf16[512,128]{1,0:T(8,128)(2,1)} %q_ref.1) | copy-start | bytes 393220
  3.5 0.9 %copy-start.7 = (bf16[512,128]{1,0:T(8,128)(2,1)S(1)}, bf16[512,128]{1,0:T(8,128)(2,1)}, u32[]{:S(2)}) copy-start(bf16[512,128]{1,0:T(8,128)(2,1)} %k_ref.1) | copy-start | bytes 393220
  4.5 0.9 %copy-start.8 = (bf16[512,128]{1,0:T(8,128)(2,1)S(1)}, bf16[512,128]{1,0:T(8,128)(2,1)}, u32[]{:S(2)}) copy-start(bf16[512,128]{1,0:T(8,128)(2,1)} %v_ref.1) | copy-start | bytes 393220
  5.4 0.9 %copy-start.9 = (bf16[512,128]{1,0:T(8,128)(2,1)S(1)}, bf16[512,128]{1,0:T(8,128)(2,1)}, u32[]{:S(2)}) copy-start(bf16[512,128]{1,0:T(8,128)(2,1)} %cot_ref.1) | copy-start | bytes 393220
  6.3 0.8 %copy-start.10 = (f32[2,64,128]{2,1,0:T(8,128)S(1)}, f32[2,64,128]{2,1,0:T(8,128)}, u32[]{:S(2)}) copy-start(f32[2,64,128]{2,1,0:T(8,128)} %constant.11.clone.turn_ref) | copy-start | bytes 196612
  7.1 0.8 %copy-start.11 = (bf16[128,256]{1,0:T(8,128)(2,1)S(1)}, bf16[128,256]{1,0:T(8,128)(2,1)}, u32[]{:S(2)}) copy-start(bf16[128,256]{1,0:T(8,128)(2,1)} %constant.8.clone.first_ref) | copy-start | bytes 196612
  7.9 0.8 %copy-start.12 = (bf16[64,384]{1,0:T(8,128)(2,1)S(1)}, bf16[64,384]{1,0:T(8,128)(2,1)}, u32[]{:S(2)}) copy-start(bf16[64,384]{1,0:T(8,128)(2,1)} %constant.10.clone.last_ref) | copy-start | bytes 147460
  68.9 0.7 copy-start.2
  69.6 0.6 copy-start.3
  70.2 0.7 copy-start.4
  70.9 0.6 copy-start.5
  71.6 0.6 copy-start.13
where the time goes:
time: 76.4 us; the launch traced here: 76 us
  Pallas kernels  62.3 us (82%)
  local copies, waits for them, and re-layouts  13 us (17%)
    pallas_call x1, Pallas kernels, on_device(): pl.pallas_call(main_kernel, out_shape=(stream, stream, stream, filt, jax....  60.2 us
    unnamed x29, local copies, waits for them, and re-layouts  11.3 us
    pallas_call x1, Pallas kernels, on_device(): pl.pallas_call(write_kernel, out_shape=(stream, stream, stream, filt, jax...  2.16 us
    pallas_call x1, local copies, waits for them, and re-layouts, on_device(): pl.pallas_call(write_kernel, out_shape=(stream, stream, stream, filt, jax...  1.66 us

commit v1 on v0

v1 whole, which is shorter than its diff:
```python
import math

import jax
import jax.numpy as jnp
import ml_dtypes
import numpy as np
from jax import lax
from jax.experimental import pallas as pl
from jax.experimental.pallas import tpu as pltpu
from jax.sharding import PartitionSpec as P

TAPS = 3
MESH = pl.DeviceIdType.MESH
BF = jnp.bfloat16
F32 = jnp.float32

S = 64
W = 128
C = 8
N = S * W
PLANE = 16
HI = 4
PARTS = (range(0, 4), range(4, 8))
VMEM_BYTES = 66_900_000


def halves(table):
    hi = table.astype(ml_dtypes.bfloat16)
    lo = (table - hi.astype(np.float64)).astype(ml_dtypes.bfloat16)
    return hi, lo


def tables():
    quarter = np.arange(S) + 0.25
    rows = 2.0 * np.pi * np.outer(quarter, np.arange(S)) / S
    twist = 2.0 * np.pi * np.outer(quarter, np.arange(W)) / N
    cols = 2.0 * np.pi * np.outer(np.arange(W), np.arange(W)) / W
    a_hi, a_lo = halves(np.concatenate([np.cos(rows), -np.sin(rows)], axis=0))
    b_hi, b_lo = halves(np.concatenate([np.cos(rows).T, -np.sin(rows).T], axis=1) / N)
    fr, fi = np.cos(cols), -np.sin(cols)
    f_hi, f_lo = halves(np.block([[fr, fi], [-fi, fr]]))
    g_hi, g_lo = halves(np.block([[fr, -fi], [fi, fr]]))
    first = np.concatenate([a_hi, a_lo, a_hi, a_lo], axis=1)
    last = np.concatenate([b_hi, b_lo, b_hi], axis=1)
    middle = np.stack([f_hi, f_lo, g_hi, g_lo])
    turn = np.stack([np.cos(twist), -np.sin(twist)]).astype(np.float32)
    return first, middle, last, turn


def split(x):
    hi = x.astype(BF)
    return hi, (x - hi.astype(F32)).astype(BF)


def dot(a, b):
    return jnp.dot(a, b, preferred_element_type=F32)


def to_rows(x):
    return jnp.concatenate([x[:, i : i + W] for i in range(0, x.shape[1], W)], axis=0)


def to_cols(x):
    return jnp.concatenate([x[i : i + S] for i in range(0, x.shape[0], S)], axis=1)


def wide(table, like):
    return jnp.concatenate([table] * (like.shape[1] // W), axis=1)


def forward(stacked, first, middle, turn):
    y = dot(first, stacked)
    yr, yi = y[:S], y[S:]
    tc, ts = wide(turn[0], yr), wide(turn[1], yr)
    turned = jnp.concatenate([to_rows(yr * tc - yi * ts), to_rows(yr * ts + yi * tc)], axis=1)
    hi, lo = split(turned)
    return dot(hi, middle[0]) + dot(lo, middle[0]) + dot(hi, middle[1])


def inverse(spec_re, spec_im, middle, last, turn):
    hi, lo = split(jnp.concatenate([spec_re, spec_im], axis=1))
    v = dot(hi, middle[2]) + dot(lo, middle[2]) + dot(hi, middle[3])
    vr, vi = to_cols(v[:, :W]), to_cols(v[:, W:])
    tc, ts = wide(turn[0], vr), wide(turn[1], vr)
    hi, lo = split(jnp.concatenate([vr * tc + vi * ts, vi * tc - vr * ts], axis=0))
    return dot(last[...], jnp.concatenate([hi, hi, lo], axis=0))


def load_signal(ref, channels):
    return jnp.concatenate([ref[pl.ds(c, S, stride=C), :] for c in channels], axis=1)


def store_signal(ref, x, channels):
    for i, c in enumerate(channels):
        ref[pl.ds(c, S, stride=C), :] = x[:, i * W : (i + 1) * W]


def row_pick(rows, lanes):
    r = lax.broadcasted_iota(jnp.int32, (8, W), 0)
    l = lax.broadcasted_iota(jnp.int32, (8, W), 1)
    hit = None
    for row, lane in zip(rows, lanes):
        one = (r == row) & (l == lane)
        hit = one if hit is None else hit | one
    return hit.astype(F32)


def pack_pair(x, lanes):
    total = None
    for b in range(4):
        part = lax.dot_general(
            row_pick((2 * b, 2 * b + 1), lanes).astype(BF),
            x[b * W : (b + 1) * W],
            (((1,), (1,)), ((), ())),
            preferred_element_type=F32,
        )
        total = part if total is None else total + part
    return total


def unpack_pair(packed, lanes):
    turned = packed.T.astype(BF)
    return jnp.concatenate(
        [dot(turned, row_pick((2 * b, 2 * b + 1), lanes).astype(BF)) for b in range(4)], axis=0
    )


def main_kernel(
    q_hbm, k_hbm, v_hbm, cot_hbm, h_hbm, a_hbm, first_hbm, mid_hbm, last_hbm, turn_hbm,
    qg_hbm, kg_hbm, vg_hbm, fg_hbm, tg_hbm,
    g_out, g_in, m_out, m_in, b_out, b_in, c_out, c_in,
    vh_out, vh_in, fh_out, fh_in, tp_out, tp_in, tz_out, tz_in,
    rows_ref, filt_ref, low_ref, hs_ref, gs_ref, ms_ref,
    q_ref, k_ref, v_ref, cot_ref, h_ref, a_ref, first_ref, mid_ref, last_ref, turn_ref,
    qg_ref, kg_ref, vg_ref, fg_ref, tg_ref,
    send_sems, recv_sems, load_sems, store_sems,
):
    loads = [
        pltpu.make_async_copy(src, dst, load_sems.at[i])
        for i, (src, dst) in enumerate((
            (h_hbm, h_ref), (first_hbm, first_ref), (turn_hbm, turn_ref), (mid_hbm, mid_ref),
            (cot_hbm, cot_ref), (q_hbm, q_ref), (v_hbm, v_ref), (a_hbm, a_ref),
            (k_hbm, k_ref), (last_hbm, last_ref),
        ))
    ]
    stores = [
        pltpu.make_async_copy(src, dst, store_sems.at[i])
        for i, (src, dst) in enumerate((
            (qg_ref, qg_hbm), (kg_ref, kg_hbm), (vg_ref, vg_hbm), (fg_ref, fg_hbm), (tg_ref, tg_hbm),
        ))
    ]
    me = lax.axis_index("seq")
    after, before = lax.rem(me + 1, S), lax.rem(me + S - 1, S)
    barrier = pltpu.get_barrier_semaphore()

    place, height = lax.rem(me, PLANE), me // PLANE

    def to_all(act):
        heights = [lax.rem(height + h, HI) * PLANE for h in (2, 1, 3, 0)]
        for base in heights[:3]:
            act(base + place)

        def one(i, carry):
            at = lax.rem(place + i, PLANE)
            for base in heights:
                act(base + at)
            return carry

        lax.fori_loop(1, PLANE, one, 0)

    to_all(
        lambda to: pl.semaphore_signal(barrier, inc=1, device_id={"seq": to}, device_id_type=MESH)
    )
    for load in loads:
        load.start()

    def remote(src, dst, index, to):
        return pltpu.make_async_remote_copy(
            src_ref=src, dst_ref=dst, send_sem=send_sems.at[index], recv_sem=recv_sems.at[index],
            device_id={"seq": to}, device_id_type=MESH,
        )

    def exchange(out, into, index, channels=range(C)):
        part = pl.ds(channels[0], len(channels))
        to_all(lambda to: remote(out.at[to, part], into.at[me, part], index, to).start())
        into[me, part] = out[me, part]

    def arrived(buffer, sem, count):
        part = buffer.at[pl.ds(0, count)]
        pltpu.make_async_copy(part, part, sem).wait()

    def exchanged(buffer, sem, channels=range(C)):
        part = buffer.at[pl.ds(0, S - 1), pl.ds(channels[0], len(channels))]
        pltpu.make_async_copy(part, part, sem).wait()

    first, turn = first_ref, turn_ref
    tiles_ref = rows_ref.reshape(S, C, W)

    with jax.named_scope("local"):
        for load in loads:
            load.wait()
        cot = cot_ref[...].astype(F32)
        g_out[...] = (cot * q_ref[...].astype(F32)).astype(BF).reshape(S, C, W)
        vh_out[...] = pack_pair(v_ref[...], (W - 2, W - 1))
        for n in range(S):
            rows_ref[n * C : (n + 1) * C, :] = h_ref[:, n * W : (n + 1) * W]
        hi, lo = split(load_signal(rows_ref, range(C)))
        hs_ref[...] = forward(jnp.concatenate([hi, hi, lo, lo], axis=0), first[...], mid_ref, turn)

    with jax.named_scope("wait_barrier"):
        pl.semaphore_wait(barrier, S - 1)

    halo_v = remote(vh_out, vh_in, 0, after)
    halo_v.start()
    with jax.named_scope("send_g"):
        for index, channels in zip((1, 8), PARTS):
            exchange(g_out, g_in, index, channels)

    value = v_ref[...].astype(F32)
    a_all = a_ref[...]
    taps = jnp.concatenate(
        [
            jnp.concatenate([a_all[:, b * W : (b + 1) * W], jnp.zeros((8 - TAPS, W), F32)], axis=0).T
            for b in range(4)
        ],
        axis=0,
    )
    with jax.named_scope("wait_halo_v"):
        halo_v.wait()
    held = jnp.where(me > 0, vh_in[...], 0.0)
    value_prev = unpack_pair(held, (W - 2, W - 1))
    lane = lax.broadcasted_iota(jnp.int32, (C * S, W), 1)

    def lagged(j):
        if j == 0:
            return value
        return jnp.where(lane < j, pltpu.roll(value_prev, j, 1), pltpu.roll(value, j, 1))

    filtered = taps[:, 0:1] * value
    for j in range(1, TAPS):
        filtered = filtered + taps[:, j : j + 1] * lagged(j)
    filt_ref[...] = filtered
    m_out[...] = (k_ref[...].astype(F32) * filtered).astype(BF).reshape(S, C, W)
    with jax.named_scope("send_m"):
        exchange(m_out, m_in, 2)

    def take(buffer, channels):
        part = pl.ds(channels[0], len(channels))
        tiles_ref[:, part, :] = buffer[:, part, :].astype(F32)
        x = load_signal(rows_ref, channels).astype(BF)
        return forward(jnp.concatenate([x, x], axis=0), first[:, : 2 * S], mid_ref, turn)

    def give(buffer, x, channels):
        part = pl.ds(channels[0], len(channels))
        store_signal(rows_ref, x, channels)
        buffer[:, part, :] = tiles_ref[:, part, :].astype(BF)

    for index, channels in zip((1, 8), PARTS):
        with jax.named_scope("wait_g"):
            exchanged(g_in, recv_sems.at[index], channels)
        grad = take(g_in, channels)
        mine = pl.ds(channels[0] * S, len(channels) * S)
        gs_ref[mine, :] = grad
        hs = hs_ref[mine, :]
        hr, hi_ = hs[:, :W], hs[:, W:]
        gr, gi = grad[:, :W], grad[:, W:]
        back = inverse(hr * gr + hi_ * gi, hr * gi - hi_ * gr, mid_ref, last_ref, turn)
        give(b_out, back, channels)
        with jax.named_scope("send_b"):
            exchange(b_out, b_in, index + 2, channels)

    with jax.named_scope("wait_m"):
        exchanged(m_in, recv_sems.at[2])
    mixed = take(m_in, range(C))
    ms_ref[...] = mixed
    hs = hs_ref[...]
    hr, hi_ = hs[:, :W], hs[:, W:]
    mr, mi = mixed[:, :W], mixed[:, W:]
    conv = inverse(mr * hr - mi * hi_, mr * hi_ + mi * hr, mid_ref, last_ref, turn)
    give(c_out, conv, range(C))
    with jax.named_scope("send_c"):
        exchange(c_out, c_in, 4)

    mixed, grad = ms_ref[...], gs_ref[...]
    mr, mi = mixed[:, :W], mixed[:, W:]
    gr, gi = grad[:, :W], grad[:, W:]
    fg = inverse(mr * gr + mi * gi, mr * gi - mi * gr, mid_ref, last_ref, turn)
    store_signal(rows_ref, fg * (1.0 / math.sqrt(N)), range(C))
    for n in range(S):
        fg_ref[:, n * W : (n + 1) * W] = rows_ref[n * C : (n + 1) * C, :]
    stores[3].start()

    with jax.named_scope("wait_b"):
        for index, channels in zip((3, 10), PARTS):
            exchanged(b_in, recv_sems.at[index], channels)
    back = b_in[...].astype(F32).reshape(S * C, W)
    low_bf = (back * k_ref[...].astype(F32)).astype(BF)
    low_ref[...] = low_bf.astype(F32)
    fh_out[...] = pack_pair(low_bf, (0, 1))
    halo_f = remote(fh_out, fh_in, 5, before)
    halo_f.start()

    low = low_ref[...]
    row8 = lax.broadcasted_iota(jnp.int32, (8, W), 0)
    partial = jnp.zeros((8, 2 * W), F32)
    for j in range(TAPS):
        pieces = split(low * lagged(j))
        for half in range(2):
            mark = (row8 == 4 * half + j).astype(BF)
            for piece in pieces:
                partial = partial + lax.dot_general(
                    mark, piece[half * 2 * W : (half + 1) * 2 * W], (((1,), (1,)), ((), ())),
                    preferred_element_type=F32,
                )
    tp_out[...] = partial
    def to_plane(i, carry):
        to = height * PLANE + lax.rem(place + i, PLANE)
        remote(tp_out, tp_in.at[place], 6, to).start()
        return carry

    with jax.named_scope("send_tp"):
        lax.fori_loop(1, PLANE, to_plane, 0)
    tp_in[place] = tp_out[...]

    kg_ref[...] = (b_in[...].astype(F32).reshape(S * C, W) * filt_ref[...]).astype(BF)
    stores[1].start()

    with jax.named_scope("wait_tp"):
        arrived(tp_in, recv_sems.at[6], PLANE - 1)
    tz_out[...] = jnp.sum(tp_in[...], axis=0)

    def to_heights(i, carry):
        to = lax.rem(height + i, HI) * PLANE + place
        remote(tz_out, tz_in.at[height], 7, to).start()
        return carry

    lax.fori_loop(1, HI, to_heights, 0)
    tz_in[height] = tz_out[...]

    with jax.named_scope("wait_halo_f"):
        halo_f.wait()
    held = jnp.where(me < S - 1, fh_in[...], 0.0)
    low_next = unpack_pair(held, (0, 1))
    value_grad = taps[:, 0:1] * low
    for j in range(1, TAPS):
        ahead = jnp.where(lane >= W - j, pltpu.roll(low_next, W - j, 1), pltpu.roll(low, W - j, 1))
        value_grad = value_grad + taps[:, j : j + 1] * ahead
    vg_ref[...] = value_grad.astype(BF)
    stores[2].start()

    with jax.named_scope("wait_c"):
        exchanged(c_in, recv_sems.at[4])
    conv = c_in[...].astype(F32).reshape(S * C, W)
    qg_ref[...] = (cot_ref[...].astype(F32) * conv).astype(BF)
    stores[0].start()

    with jax.named_scope("wait_tz"):
        arrived(tz_in, recv_sems.at[7], HI - 1)
    sums = jnp.sum(tz_in[...], axis=0) * (1.0 / math.sqrt(N))
    tg_ref[:, : 2 * W] = sums[:TAPS]
    tg_ref[:, 2 * W :] = sums[4 : 4 + TAPS]
    stores[4].start()

    for index, channels in zip((1, 8), PARTS):
        exchanged(g_out, send_sems.at[index], channels)
        exchanged(b_out, send_sems.at[index + 2], channels)
    exchanged(m_out, send_sems.at[2])
    exchanged(c_out, send_sems.at[4])
    arrived(tp_in, send_sems.at[6], PLANE - 1)
    arrived(tz_in, send_sems.at[7], HI - 1)
    for store in stores:
        store.wait()


def write_kernel(*refs):
    ins, outs, held, sems, more = refs[:5], refs[5:10], refs[10:15], refs[15], refs[16]
    loads = [
        pltpu.make_async_copy(src, dst, sems.at[i]) for i, (src, dst) in enumerate(zip(ins, held))
    ]
    stores = [
        pltpu.make_async_copy(src, dst, more.at[i]) for i, (src, dst) in enumerate(zip(held, outs))
    ]
    for load in loads:
        load.start()
    for load, store in zip(loads, stores):
        load.wait()
        store.start()
    for store in stores:
        store.wait()


def on_device(query_gate, key_gate, value_in, cotangent, long_filter, short_taps):
    rows, width = key_gate.shape
    first, middle, last, turn = (jnp.asarray(t) for t in tables())
    hbm = pl.BlockSpec(memory_space=pltpu.HBM)
    stream = jax.ShapeDtypeStruct((rows, width), BF)
    filt = jax.ShapeDtypeStruct((C, N), F32)
    shapes = (stream, stream, stream, filt, jax.ShapeDtypeStruct((TAPS, rows), F32))
    operands = (query_gate, key_gate, value_in, cotangent, long_filter, short_taps.T, first, middle, last, turn)
    outs = pl.pallas_call(
        main_kernel,
        out_shape=shapes,
        in_specs=[hbm] * 10,
        out_specs=(hbm,) * 5,
        scratch_shapes=[pltpu.VMEM((S, C, W), BF)] * 8
        + [pltpu.VMEM((8, W), F32)] * 4
        + [
            pltpu.VMEM((8, 2 * W), F32),
            pltpu.VMEM((PLANE, 8, 2 * W), F32),
            pltpu.VMEM((8, 2 * W), F32),
            pltpu.VMEM((HI, 8, 2 * W), F32),
            pltpu.VMEM((S * C, W), F32),
            pltpu.VMEM((S * C, W), F32),
            pltpu.VMEM((S * C, W), F32),
            pltpu.VMEM((S * C, 2 * W), F32),
            pltpu.VMEM((S * C, 2 * W), F32),
            pltpu.VMEM((S * C, 2 * W), F32),
        ]
        + [pltpu.VMEM(x.shape, x.dtype) for x in (*operands, *shapes)]
        + [
            pltpu.SemaphoreType.DMA((11,)),
            pltpu.SemaphoreType.DMA((11,)),
            pltpu.SemaphoreType.DMA((len(operands),)),
            pltpu.SemaphoreType.DMA((len(shapes),)),
        ],
        compiler_params=pltpu.CompilerParams(
            collective_id=0, has_side_effects=True, vmem_limit_bytes=VMEM_BYTES
        ),
        name="exchange",
    )(*operands)
    *streams, tap_sums = pl.pallas_call(
        write_kernel,
        out_shape=shapes,
        in_specs=[hbm] * 5,
        out_specs=(hbm,) * 5,
        scratch_shapes=[pltpu.VMEM(x.shape, x.dtype) for x in shapes]
        + [pltpu.SemaphoreType.DMA((5,)), pltpu.SemaphoreType.DMA((5,))],
        compiler_params=pltpu.CompilerParams(vmem_limit_bytes=VMEM_BYTES),
        name="write",
    )(*outs)
    return (*streams, tap_sums.T)


def solution(mesh):
    spec = P("chan", "seq")
    owned = P(("chan", "seq"), None)
    taps = P("chan", None)
    return jax.shard_map(
        on_device,
        mesh=mesh,
        in_specs=(spec, spec, spec, spec, owned, taps),
        out_specs=(spec, spec, spec, owned, taps),
        check_vma=False,
    )
```

time: 76.4 us -> 62.7 us (0.82)
  the two profiles are of different devices: /device:TPU:64 before, /device:TPU:8 now
where the time goes in v1:
time: 62.7 us; the launch traced here: 62.5 us
  Pallas kernels  61.9 us (99%)
  between operations  0.64 us (1%)
    pallas_call x1, Pallas kernels, on_device(): pl.pallas_call(main_kernel, out_shape=shapes, in_specs=[hbm] * 10, out_sp...  59.9 us
    pallas_call x1, Pallas kernels, on_device(): pl.pallas_call(write_kernel, out_shape=shapes, in_specs=[hbm] * 5, out_sp...  1.94 us

profile of v1, /device:TPU:8, one launch (start us, length us, event | category | flops | bytes accessed | tf_op | source)
XLA Modules:
  0.0 62.5 jit_solution(12320833779278969971)
XLA Ops:
  0.6 59.9 %exchange.1 = (bf16[512,128]{1,0:T(8,128)(2,1)}, bf16[512,128]{1,0:T(8,128)(2,1)}, bf16[512,128]{1,0:T(8,128)(2,1)}, f32[8,8192]{1,0:T(8,128)}, f32[3,512]{1,0:T(4,128)}) custom-call(bf16[512,128]{1,0:T(8,128)(2,1)} %q_hbm.1, bf16[512,128]{1,0:T(8,128)(2,1)} %k_hbm.1, bf16[512,128]{1,0:T(8,128)(2,1)} %v_hbm.1, bf16[512,128]{1,0:T(8,128)(2,1)} %cot_hbm.1, ...), custom_call_target="tpu_custom_call" | custom-call | tf_op jit(solution)/shard_map/exchange/pallas_call | solution.py:400
  60.6 1.9 %write.1 = (bf16[512,128]{1,0:T(8,128)(2,1)}, bf16[512,128]{1,0:T(8,128)(2,1)}, bf16[512,128]{1,0:T(8,128)(2,1)}, f32[8,8192]{1,0:T(8,128)}, f32[3,512]{1,0:T(4,128)}) custom-call(bf16[512,128]{1,0:T(8,128)(2,1)} %get-tuple-element.15.refs_0_, bf16[512,128]{1,0:T(8,128)(2,1)} %get-tuple-element.16.refs_1_, bf16[512,128]{1,0:T(8,128)(2,1)} %get-tuple-element.17.refs_2_, ...), custom_call_target="tpu_custom_call" | custom-call | tf_op jit(solution)/shard_map/write/pallas_call | solution.py:431

commit v2 on v1

--- a/solution.py
+++ b/solution.py
@@ -20,8 +20,13 @@
 N = S * W
 PLANE = 16
 HI = 4
-PARTS = (range(0, 4), range(4, 8))
-VMEM_BYTES = 66_900_000
+PARTS = (range(0, 4), range(4, 6), range(6, 8))
+WHOLE = range(C)
+PLANE_SUM, HEIGHT_SUM, VALUE_HALO, GRAD_HALO, MIXED, CONV, GRAD = range(7)
+BACK = GRAD + len(PARTS)
+SEMAPHORES = BACK + len(PARTS)
+VMEM_BYTES = 55_820_000
+WRITE_BYTES = 4_000_000
 
 
 def halves(table):
@@ -40,11 +45,17 @@
     fr, fi = np.cos(cols), -np.sin(cols)
     f_hi, f_lo = halves(np.block([[fr, fi], [-fi, fr]]))
     g_hi, g_lo = halves(np.block([[fr, -fi], [fi, fr]]))
-    first = np.concatenate([a_hi, a_lo, a_hi, a_lo], axis=1)
-    last = np.concatenate([b_hi, b_lo, b_hi], axis=1)
-    middle = np.stack([f_hi, f_lo, g_hi, g_lo])
-    turn = np.stack([np.cos(twist), -np.sin(twist)]).astype(np.float32)
-    return first, middle, last, turn
+    turn = np.concatenate([np.cos(twist), -np.sin(twist)], axis=1)
+    turn_hi, turn_lo = halves(turn)
+    turn_rest = (turn - turn_hi.astype(np.float64) - turn_lo.astype(np.float64)).astype(ml_dtypes.bfloat16)
+    return np.concatenate(
+        [
+            f_hi, f_lo, g_hi, g_lo,
+            np.concatenate([a_hi, a_lo, a_hi, a_lo], axis=1),
+            np.concatenate([b_hi, b_lo], axis=1), turn_hi, turn_lo, turn_rest,
+        ],
+        axis=0,
+    )
 
 
 def split(x):
@@ -74,16 +85,16 @@
     tc, ts = wide(turn[0], yr), wide(turn[1], yr)
     turned = jnp.concatenate([to_rows(yr * tc - yi * ts), to_rows(yr * ts + yi * tc)], axis=1)
     hi, lo = split(turned)
-    return dot(hi, middle[0]) + dot(lo, middle[0]) + dot(hi, middle[1])
+    return dot(hi, middle(0)) + dot(lo, middle(0)) + dot(hi, middle(1))
 
 
 def inverse(spec_re, spec_im, middle, last, turn):
     hi, lo = split(jnp.concatenate([spec_re, spec_im], axis=1))
-    v = dot(hi, middle[2]) + dot(lo, middle[2]) + dot(hi, middle[3])
+    v = dot(hi, middle(2)) + dot(lo, middle(2)) + dot(hi, middle(3))
     vr, vi = to_cols(v[:, :W]), to_cols(v[:, W:])
     tc, ts = wide(turn[0], vr), wide(turn[1], vr)
     hi, lo = split(jnp.concatenate([vr * tc + vi * ts, vi * tc - vr * ts], axis=0))
-    return dot(last[...], jnp.concatenate([hi, hi, lo], axis=0))
+    return dot(last(), jnp.concatenate([hi, hi, lo], axis=0))
 
 
 def load_signal(ref, channels):
@@ -126,27 +137,19 @@
 
 
 def main_kernel(
-    q_hbm, k_hbm, v_hbm, cot_hbm, h_hbm, a_hbm, first_hbm, mid_hbm, last_hbm, turn_hbm,
-    qg_hbm, kg_hbm, vg_hbm, fg_hbm, tg_hbm,
+    q_hbm, k_hbm, v_hbm, cot_hbm, h_hbm, a_hbm, table_hbm,
+    qg_ref, kg_ref, vg_ref, fg_ref, fg_more, tg_ref,
     g_out, g_in, m_out, m_in, b_out, b_in, c_out, c_in,
     vh_out, vh_in, fh_out, fh_in, tp_out, tp_in, tz_out, tz_in,
-    rows_ref, filt_ref, low_ref, hs_ref, gs_ref, ms_ref,
-    q_ref, k_ref, v_ref, cot_ref, h_ref, a_ref, first_ref, mid_ref, last_ref, turn_ref,
-    qg_ref, kg_ref, vg_ref, fg_ref, tg_ref,
-    send_sems, recv_sems, load_sems, store_sems,
+    rows_ref, filt_ref, low_ref, lag_ref, hs_ref, gs_ref, ms_ref,
+    q_ref, k_ref, v_ref, cot_ref, h_ref, a_ref, table_ref, turn_ref,
+    send_sems, recv_sems, load_sems,
 ):
     loads = [
         pltpu.make_async_copy(src, dst, load_sems.at[i])
         for i, (src, dst) in enumerate((
-            (h_hbm, h_ref), (first_hbm, first_ref), (turn_hbm, turn_ref), (mid_hbm, mid_ref),
-            (cot_hbm, cot_ref), (q_hbm, q_ref), (v_hbm, v_ref), (a_hbm, a_ref),
-            (k_hbm, k_ref), (last_hbm, last_ref),
-        ))
-    ]
-    stores = [
-        pltpu.make_async_copy(src, dst, store_sems.at[i])
-        for i, (src, dst) in enumerate((
-            (qg_ref, qg_hbm), (kg_ref, kg_hbm), (vg_ref, vg_hbm), (fg_ref, fg_hbm), (tg_ref, tg_hbm),
+            (h_hbm, h_ref), (table_hbm, table_ref), (cot_hbm, cot_ref), (q_hbm, q_ref),
+            (v_hbm, v_ref), (a_hbm, a_ref), (k_hbm, k_ref),
         ))
     ]
     me = lax.axis_index("seq")
@@ -180,7 +183,7 @@
             device_id={"seq": to}, device_id_type=MESH,
         )
 
-    def exchange(out, into, index, channels=range(C)):
+    def exchange(out, into, index, channels):
         part = pl.ds(channels[0], len(channels))
         to_all(lambda to: remote(out.at[to, part], into.at[me, part], index, to).start())
         into[me, part] = out[me, part]
@@ -189,16 +192,29 @@
         part = buffer.at[pl.ds(0, count)]
         pltpu.make_async_copy(part, part, sem).wait()
 
-    def exchanged(buffer, sem, channels=range(C)):
+    def exchanged(buffer, sem, channels):
         part = buffer.at[pl.ds(0, S - 1), pl.ds(channels[0], len(channels))]
         pltpu.make_async_copy(part, part, sem).wait()
 
-    first, turn = first_ref, turn_ref
+    first = table_ref.at[pl.ds(1024, 2 * S)]
+    turn = turn_ref
+
+    def mid_ref(i):
+        return table_ref[256 * i : 256 * (i + 1), :]
+
+    def last_ref():
+        back = table_ref[1152 : 1152 + S, :]
+        return jnp.concatenate([back, back[:, : 2 * S]], axis=1)
+
     tiles_ref = rows_ref.reshape(S, C, W)
 
     with jax.named_scope("local"):
         for load in loads:
             load.wait()
+        pieces = [table_ref[1216 + i * S : 1216 + (i + 1) * S, :].astype(F32) for i in range(3)]
+        turned = pieces[0] + pieces[1] + pieces[2]
+        turn_ref[0] = turned[:, :W]
+        turn_ref[1] = turned[:, W:]
         cot = cot_ref[...].astype(F32)
         g_out[...] = (cot * q_ref[...].astype(F32)).astype(BF).reshape(S, C, W)
         vh_out[...] = pack_pair(v_ref[...], (W - 2, W - 1))
@@ -210,11 +226,11 @@
     with jax.named_scope("wait_barrier"):
         pl.semaphore_wait(barrier, S - 1)
 
-    halo_v = remote(vh_out, vh_in, 0, after)
+    halo_v = remote(vh_out, vh_in, VALUE_HALO, after)
     halo_v.start()
     with jax.named_scope("send_g"):
-        for index, channels in zip((1, 8), PARTS):
-            exchange(g_out, g_in, index, channels)
+        for i, channels in enumerate(PARTS):
+            exchange(g_out, g_in, GRAD + i, channels)
 
     value = v_ref[...].astype(F32)
     a_all = a_ref[...]
@@ -232,17 +248,17 @@
     lane = lax.broadcasted_iota(jnp.int32, (C * S, W), 1)
 
     def lagged(j):
-        if j == 0:
-            return value
         return jnp.where(lane < j, pltpu.roll(value_prev, j, 1), pltpu.roll(value, j, 1))
 
     filtered = taps[:, 0:1] * value
+    lag_ref[0] = value
     for j in range(1, TAPS):
-        filtered = filtered + taps[:, j : j + 1] * lagged(j)
+        lag_ref[j] = lagged(j)
+        filtered = filtered + taps[:, j : j + 1] * lag_ref[j]
     filt_ref[...] = filtered
     m_out[...] = (k_ref[...].astype(F32) * filtered).astype(BF).reshape(S, C, W)
     with jax.named_scope("send_m"):
-        exchange(m_out, m_in, 2)
+        exchange(m_out, m_in, MIXED, WHOLE)
 
     def take(buffer, channels):
         part = pl.ds(channels[0], len(channels))
@@ -255,9 +271,9 @@
         store_signal(rows_ref, x, channels)
         buffer[:, part, :] = tiles_ref[:, part, :].astype(BF)
 
-    for index, channels in zip((1, 8), PARTS):
+    for i, channels in enumerate(PARTS):
         with jax.named_scope("wait_g"):
-            exchanged(g_in, recv_sems.at[index], channels)
+            exchanged(g_in, recv_sems.at[GRAD + i], channels)
         grad = take(g_in, channels)
         mine = pl.ds(channels[0] * S, len(channels) * S)
         gs_ref[mine, :] = grad
@@ -267,19 +283,19 @@
         back = inverse(hr * gr + hi_ * gi, hr * gi - hi_ * gr, mid_ref, last_ref, turn)
         give(b_out, back, channels)
         with jax.named_scope("send_b"):
-            exchange(b_out, b_in, index + 2, channels)
+            exchange(b_out, b_in, BACK + i, channels)
 
     with jax.named_scope("wait_m"):
-        exchanged(m_in, recv_sems.at[2])
-    mixed = take(m_in, range(C))
+        exchanged(m_in, recv_sems.at[MIXED], WHOLE)
+    mixed = take(m_in, WHOLE)
     ms_ref[...] = mixed
     hs = hs_ref[...]
     hr, hi_ = hs[:, :W], hs[:, W:]
     mr, mi = mixed[:, :W], mixed[:, W:]
     conv = inverse(mr * hr - mi * hi_, mr * hi_ + mi * hr, mid_ref, last_ref, turn)
-    give(c_out, conv, range(C))
+    give(c_out, conv, WHOLE)
     with jax.named_scope("send_c"):
-        exchange(c_out, c_in, 4)
+        exchange(c_out, c_in, CONV, WHOLE)
 
     mixed, grad = ms_ref[...], gs_ref[...]
     mr, mi = mixed[:, :W], mixed[:, W:]
@@ -287,24 +303,20 @@
     fg = inverse(mr * gr + mi * gi, mr * gi - mi * gr, mid_ref, last_ref, turn)
     store_signal(rows_ref, fg * (1.0 / math.sqrt(N)), range(C))
     for n in range(S):
-        fg_ref[:, n * W : (n + 1) * W] = rows_ref[n * C : (n + 1) * C, :]
-    stores[3].start()
+        part, at = (fg_ref, n * W) if n < S // 2 else (fg_more, (n - S // 2) * W)
+        part[:, at : at + W] = rows_ref[n * C : (n + 1) * C, :]
 
     with jax.named_scope("wait_b"):
-        for index, channels in zip((3, 10), PARTS):
-            exchanged(b_in, recv_sems.at[index], channels)
+        for i, channels in enumerate(PARTS):
+            exchanged(b_in, recv_sems.at[BACK + i], channels)
     back = b_in[...].astype(F32).reshape(S * C, W)
     low_bf = (back * k_ref[...].astype(F32)).astype(BF)
     low_ref[...] = low_bf.astype(F32)
-    fh_out[...] = pack_pair(low_bf, (0, 1))
-    halo_f = remote(fh_out, fh_in, 5, before)
-    halo_f.start()
-
     low = low_ref[...]
     row8 = lax.broadcasted_iota(jnp.int32, (8, W), 0)
     partial = jnp.zeros((8, 2 * W), F32)
     for j in range(TAPS):
-        pieces = split(low * lagged(j))
+        pieces = split(low * lag_ref[j])
         for half in range(2):
             mark = (row8 == 4 * half + j).astype(BF)
             for piece in pieces:
@@ -315,23 +327,25 @@
     tp_out[...] = partial
     def to_plane(i, carry):
         to = height * PLANE + lax.rem(place + i, PLANE)
-        remote(tp_out, tp_in.at[place], 6, to).start()
+        remote(tp_out, tp_in.at[place], PLANE_SUM, to).start()
         return carry
 
     with jax.named_scope("send_tp"):
         lax.fori_loop(1, PLANE, to_plane, 0)
     tp_in[place] = tp_out[...]
 
+    fh_out[...] = pack_pair(low_bf, (0, 1))
+    halo_f = remote(fh_out, fh_in, GRAD_HALO, before)
+    halo_f.start()
     kg_ref[...] = (b_in[...].astype(F32).reshape(S * C, W) * filt_ref[...]).astype(BF)
-    stores[1].start()
 
     with jax.named_scope("wait_tp"):
-        arrived(tp_in, recv_sems.at[6], PLANE - 1)
+        arrived(tp_in, recv_sems.at[PLANE_SUM], PLANE - 1)
     tz_out[...] = jnp.sum(tp_in[...], axis=0)
 
     def to_heights(i, carry):
         to = lax.rem(height + i, HI) * PLANE + place
-        remote(tz_out, tz_in.at[height], 7, to).start()
+        remote(tz_out, tz_in.at[height], HEIGHT_SUM, to).start()
         return carry
 
     lax.fori_loop(1, HI, to_heights, 0)
@@ -346,62 +360,54 @@
         ahead = jnp.where(lane >= W - j, pltpu.roll(low_next, W - j, 1), pltpu.roll(low, W - j, 1))
         value_grad = value_grad + taps[:, j : j + 1] * ahead
     vg_ref[...] = value_grad.astype(BF)
-    stores[2].start()
 
     with jax.named_scope("wait_c"):
-        exchanged(c_in, recv_sems.at[4])
+        exchanged(c_in, recv_sems.at[CONV], WHOLE)
     conv = c_in[...].astype(F32).reshape(S * C, W)
     qg_ref[...] = (cot_ref[...].astype(F32) * conv).astype(BF)
-    stores[0].start()
 
     with jax.named_scope("wait_tz"):
-        arrived(tz_in, recv_sems.at[7], HI - 1)
+        arrived(tz_in, recv_sems.at[HEIGHT_SUM], HI - 1)
     sums = jnp.sum(tz_in[...], axis=0) * (1.0 / math.sqrt(N))
     tg_ref[:, : 2 * W] = sums[:TAPS]
     tg_ref[:, 2 * W :] = sums[4 : 4 + TAPS]
-    stores[4].start()
-
-    for index, channels in zip((1, 8), PARTS):
-        exchanged(g_out, send_sems.at[index], channels)
-        exchanged(b_out, send_sems.at[index + 2], channels)
-    exchanged(m_out, send_sems.at[2])
-    exchanged(c_out, send_sems.at[4])
-    arrived(tp_in, send_sems.at[6], PLANE - 1)
-    arrived(tz_in, send_sems.at[7], HI - 1)
-    for store in stores:
-        store.wait()
-
-
-def write_kernel(*refs):
-    ins, outs, held, sems, more = refs[:5], refs[5:10], refs[10:15], refs[15], refs[16]
-    loads = [
-        pltpu.make_async_copy(src, dst, sems.at[i]) for i, (src, dst) in enumerate(zip(ins, held))
-    ]
-    stores = [
-        pltpu.make_async_copy(src, dst, more.at[i]) for i, (src, dst) in enumerate(zip(held, outs))
-    ]
-    for load in loads:
-        load.start()
-    for load, store in zip(loads, stores):
-        load.wait()
-        store.start()
-    for store in stores:
-        store.wait()
+
+    for i, channels in enumerate(PARTS):
+        exchanged(g_out, send_sems.at[GRAD + i], channels)
+        exchanged(b_out, send_sems.at[BACK + i], channels)
+    exchanged(m_out, send_sems.at[MIXED], WHOLE)
+    exchanged(c_out, send_sems.at[CONV], WHOLE)
+    arrived(tp_in, send_sems.at[PLANE_SUM], PLANE - 1)
+    arrived(tz_in, send_sems.at[HEIGHT_SUM], HI - 1)
+
+
+def write_kernel(qg, kg, vg, fg, fg_more, tg, qg_out, kg_out, vg_out, fg_out, tg_out, sems):
+    pairs = (
+        (qg, qg_out), (kg, kg_out), (vg, vg_out), (tg, tg_out),
+        (fg, fg_out.at[:, pl.ds(0, N // 2)]), (fg_more, fg_out.at[:, pl.ds(N // 2, N // 2)]),
+    )
+    copies = [pltpu.make_async_copy(src, dst, sems.at[i]) for i, (src, dst) in enumerate(pairs)]
+    for copy in copies:
+        copy.start()
+    for copy in copies:
+        copy.wait()
 
 
 def on_device(query_gate, key_gate, value_in, cotangent, long_filter, short_taps):
     rows, width = key_gate.shape
-    first, middle, last, turn = (jnp.asarray(t) for t in tables())
+    table = jnp.asarray(tables())
     hbm = pl.BlockSpec(memory_space=pltpu.HBM)
+    vmem = pl.BlockSpec(memory_space=pltpu.VMEM)
     stream = jax.ShapeDtypeStruct((rows, width), BF)
     filt = jax.ShapeDtypeStruct((C, N), F32)
-    shapes = (stream, stream, stream, filt, jax.ShapeDtypeStruct((TAPS, rows), F32))
-    operands = (query_gate, key_gate, value_in, cotangent, long_filter, short_taps.T, first, middle, last, turn)
+    half = jax.ShapeDtypeStruct((C, N // 2), F32)
+    tap_rows = jax.ShapeDtypeStruct((TAPS, rows), F32)
+    operands = (query_gate, key_gate, value_in, cotangent, long_filter, short_taps.T, table)
     outs = pl.pallas_call(
         main_kernel,
-        out_shape=shapes,
-        in_specs=[hbm] * 10,
-        out_specs=(hbm,) * 5,
+        out_shape=(stream, stream, stream, half, half, tap_rows),
+        in_specs=[hbm] * len(operands),
+        out_specs=(vmem,) * 6,
         scratch_shapes=[pltpu.VMEM((S, C, W), BF)] * 8
         + [pltpu.VMEM((8, W), F32)] * 4
         + [
@@ -412,16 +418,17 @@
             pltpu.VMEM((S * C, W), F32),
             pltpu.VMEM((S * C, W), F32),
             pltpu.VMEM((S * C, W), F32),
+            pltpu.VMEM((TAPS, S * C, W), F32),
             pltpu.VMEM((S * C, 2 * W), F32),
             pltpu.VMEM((S * C, 2 * W), F32),
             pltpu.VMEM((S * C, 2 * W), F32),
         ]
-        + [pltpu.VMEM(x.shape, x.dtype) for x in (*operands, *shapes)]
+        + [pltpu.VMEM(x.shape, x.dtype) for x in operands]
+        + [pltpu.VMEM((2, S, W), F32)]
         + [
-            pltpu.SemaphoreType.DMA((11,)),
-            pltpu.SemaphoreType.DMA((11,)),
+            pltpu.SemaphoreType.DMA((SEMAPHORES,)),
+            pltpu.SemaphoreType.DMA((SEMAPHORES,)),
             pltpu.SemaphoreType.DMA((len(operands),)),
-            pltpu.SemaphoreType.DMA((len(shapes),)),
         ],
         compiler_params=pltpu.CompilerParams(
             collective_id=0, has_side_effects=True, vmem_limit_bytes=VMEM_BYTES
@@ -430,12 +437,11 @@
     )(*operands)
     *streams, tap_sums = pl.pallas_call(
         write_kernel,
-        out_shape=shapes,
-        in_specs=[hbm] * 5,
+        out_shape=(stream, stream, stream, filt, tap_rows),
+        in_specs=[vmem] * 6,
         out_specs=(hbm,) * 5,
-        scratch_shapes=[pltpu.VMEM(x.shape, x.dtype) for x in shapes]
-        + [pltpu.SemaphoreType.DMA((5,)), pltpu.SemaphoreType.DMA((5,))],
-        compiler_params=pltpu.CompilerParams(vmem_limit_bytes=VMEM_BYTES),
+        scratch_shapes=[pltpu.SemaphoreType.DMA((6,))],
+        compiler_params=pltpu.CompilerParams(vmem_limit_bytes=WRITE_BYTES),
         name="write",
     )(*outs)
     return (*streams, tap_sums.T)

time: 62.7 us -> 60.2 us (0.960)
  the two profiles are of different devices: /device:TPU:8 before, /device:TPU:32 now
where the time goes in v2:
time: 60.2 us; the launch traced here: 60 us
  Pallas kernels  58.7 us (98%)
  local copies, waits for them, and re-layouts  0.69 us (1%)
  between operations  0.65 us (1%)
    pallas_call x1, Pallas kernels, on_device(): pl.pallas_call(main_kernel, out_shape=(stream, stream, stream, half, half...  57.8 us

profile of v2, /device:TPU:32, one launch (start us, length us, event | category | flops | bytes accessed | tf_op | source)
XLA Modules:
  0.0 60.0 jit_solution(17623438690951914006)
XLA Ops:
  0.6 0.0 copy-start
  0.6 0.7 %copy-done = f32[512,3]{0,1:T(4,128)S(1)} copy-done((f32[512,3]{0,1:T(4,128)S(1)}, f32[512,3]{0,1:T(4,128)}, u32[]{:S(2)}) %copy-start) | copy-done | bytes 6168
  1.3 57.8 %exchange.1 = (bf16[512,128]{1,0:T(8,128)(2,1)S(1)}, bf16[512,128]{1,0:T(8,128)(2,1)S(1)}, bf16[512,128]{1,0:T(8,128)(2,1)S(1)}, f32[8,4096]{1,0:T(8,128)S(1)}, ...) custom-call(bf16[512,128]{1,0:T(8,128)(2,1)} %q_hbm.1, bf16[512,128]{1,0:T(8,128)(2,1)} %k_hbm.1, bf16[512,128]{1,0:T(8,128)(2,1)} %v_hbm.1, ...), custom_call_target="tpu_custom_call" | custom-call | tf_op jit(solution)/shard_map/exchange/pallas_call | solution.py:406
  59.1 0.9 %write.1 = (bf16[512,128]{1,0:T(8,128)(2,1)}, bf16[512,128]{1,0:T(8,128)(2,1)}, bf16[512,128]{1,0:T(8,128)(2,1)}, f32[8,8192]{1,0:T(8,128)}, f32[3,512]{1,0:T(4,128)}) custom-call(bf16[512,128]{1,0:T(8,128)(2,1)S(1)} %get-tuple-element.16.qg, bf16[512,128]{1,0:T(8,128)(2,1)S(1)} %get-tuple-element.17.kg, bf16[512,128]{1,0:T(8,128)(2,1)S(1)} %get-tuple-element.18.vg, ...), custom_call_target="tpu_custom_call" | custom-call | tf_op jit(solution)/shard_map/write/pallas_call | solution.py:438
Async XLA Ops:
  0.6 0.7 %copy-start = (f32[512,3]{0,1:T(4,128)S(1)}, f32[512,3]{0,1:T(4,128)}, u32[]{:S(2)}) copy-start(f32[512,3]{0,1:T(4,128)} %param.12) | copy-start | bytes 18436

commit v3 on v2

--- a/solution.py
+++ b/solution.py
@@ -296,15 +296,6 @@
     give(c_out, conv, WHOLE)
     with jax.named_scope("send_c"):
         exchange(c_out, c_in, CONV, WHOLE)
-
-    mixed, grad = ms_ref[...], gs_ref[...]
-    mr, mi = mixed[:, :W], mixed[:, W:]
-    gr, gi = grad[:, :W], grad[:, W:]
-    fg = inverse(mr * gr + mi * gi, mr * gi - mi * gr, mid_ref, last_ref, turn)
-    store_signal(rows_ref, fg * (1.0 / math.sqrt(N)), range(C))
-    for n in range(S):
-        part, at = (fg_ref, n * W) if n < S // 2 else (fg_more, (n - S // 2) * W)
-        part[:, at : at + W] = rows_ref[n * C : (n + 1) * C, :]
 
     with jax.named_scope("wait_b"):
         for i, channels in enumerate(PARTS):
@@ -338,6 +329,15 @@
     halo_f = remote(fh_out, fh_in, GRAD_HALO, before)
     halo_f.start()
     kg_ref[...] = (b_in[...].astype(F32).reshape(S * C, W) * filt_ref[...]).astype(BF)
+
+    mixed, grad = ms_ref[...], gs_ref[...]
+    mr, mi = mixed[:, :W], mixed[:, W:]
+    gr, gi = grad[:, :W], grad[:, W:]
+    fg = inverse(mr * gr + mi * gi, mr * gi - mi * gr, mid_ref, last_ref, turn)
+    store_signal(rows_ref, fg * (1.0 / math.sqrt(N)), range(C))
+    for n in range(S):
+        part, at = (fg_ref, n * W) if n < S // 2 else (fg_more, (n - S // 2) * W)
+        part[:, at : at + W] = rows_ref[n * C : (n + 1) * C, :]
 
     with jax.named_scope("wait_tp"):
         arrived(tp_in, recv_sems.at[PLANE_SUM], PLANE - 1)

time: 60.2 us -> 60.2 us (level)
  no operation moved by 1% of the time
where the time goes in v3:
time: 60.2 us; the launch traced here: 60 us
  Pallas kernels  58.7 us (98%)
  local copies, waits for them, and re-layouts  0.69 us (1%)
  between operations  0.65 us (1%)
    pallas_call x1, Pallas kernels, on_device(): pl.pallas_call(main_kernel, out_shape=(stream, stream, stream, half, half...  57.8 us

profile of v3, /device:TPU:32, one launch (start us, length us, event | category | flops | bytes accessed | tf_op | source)
XLA Modules:
  0.0 60.0 jit_solution(5296258771008156117)
XLA Ops:
  0.6 0.0 copy-start
  0.6 0.7 %copy-done = f32[512,3]{0,1:T(4,128)S(1)} copy-done((f32[512,3]{0,1:T(4,128)S(1)}, f32[512,3]{0,1:T(4,128)}, u32[]{:S(2)}) %copy-start) | copy-done | bytes 6168
  1.3 57.8 %exchange.1 = (bf16[512,128]{1,0:T(8,128)(2,1)S(1)}, bf16[512,128]{1,0:T(8,128)(2,1)S(1)}, bf16[512,128]{1,0:T(8,128)(2,1)S(1)}, f32[8,4096]{1,0:T(8,128)S(1)}, ...) custom-call(bf16[512,128]{1,0:T(8,128)(2,1)} %q_hbm.1, bf16[512,128]{1,0:T(8,128)(2,1)} %k_hbm.1, bf16[512,128]{1,0:T(8,128)(2,1)} %v_hbm.1, ...), custom_call_target="tpu_custom_call" | custom-call | tf_op jit(solution)/shard_map/exchange/pallas_call | solution.py:406
  59.1 0.9 %write.1 = (bf16[512,128]{1,0:T(8,128)(2,1)}, bf16[512,128]{1,0:T(8,128)(2,1)}, bf16[512,128]{1,0:T(8,128)(2,1)}, f32[8,8192]{1,0:T(8,128)}, f32[3,512]{1,0:T(4,128)}) custom-call(bf16[512,128]{1,0:T(8,128)(2,1)S(1)} %get-tuple-element.16.qg, bf16[512,128]{1,0:T(8,128)(2,1)S(1)} %get-tuple-element.17.kg, bf16[512,128]{1,0:T(8,128)(2,1)S(1)} %get-tuple-element.18.vg, ...), custom_call_target="tpu_custom_call" | custom-call | tf_op jit(solution)/shard_map/write/pallas_call | solution.py:438
Async XLA Ops:
  0.6 0.7 %copy-start = (f32[512,3]{0,1:T(4,128)S(1)}, f32[512,3]{0,1:T(4,128)}, u32[]{:S(2)}) copy-start(f32[512,3]{0,1:T(4,128)} %param.12) | copy-start | bytes 18436

commit v4 on v2

--- a/solution.py
+++ b/solution.py
@@ -325,13 +325,11 @@
                     preferred_element_type=F32,
                 )
     tp_out[...] = partial
-    def to_plane(i, carry):
-        to = height * PLANE + lax.rem(place + i, PLANE)
-        remote(tp_out, tp_in.at[place], PLANE_SUM, to).start()
-        return carry
-
     with jax.named_scope("send_tp"):
-        lax.fori_loop(1, PLANE, to_plane, 0)
+        steps = [(dx, dy) for dx in range(4) for dy in range(4) if dx or dy]
+        for dx, dy in sorted(steps, key=lambda d: -sum(min(n, 4 - n) for n in d)):
+            at = lax.rem(place // 4 + dx, 4) * 4 + lax.rem(place + dy, 4)
+            remote(tp_out, tp_in.at[place], PLANE_SUM, height * PLANE + at).start()
     tp_in[place] = tp_out[...]
 
     fh_out[...] = pack_pair(low_bf, (0, 1))
@@ -343,12 +341,9 @@
         arrived(tp_in, recv_sems.at[PLANE_SUM], PLANE - 1)
     tz_out[...] = jnp.sum(tp_in[...], axis=0)
 
-    def to_heights(i, carry):
-        to = lax.rem(height + i, HI) * PLANE + place
+    for h in (2, 1, 3):
+        to = lax.rem(height + h, HI) * PLANE + place
         remote(tz_out, tz_in.at[height], HEIGHT_SUM, to).start()
-        return carry
-
-    lax.fori_loop(1, HI, to_heights, 0)
     tz_in[height] = tz_out[...]
 
     with jax.named_scope("wait_halo_f"):

time: 60.2 us -> 60.1 us (level)
  no operation moved by 1% of the time
where the time goes in v4:
time: 60.1 us; the launch traced here: 59.9 us
  Pallas kernels  58.6 us (98%)
  local copies, waits for them, and re-layouts  0.69 us (1%)
  between operations  0.65 us (1%)
    pallas_call x1, Pallas kernels, on_device(): pl.pallas_call(main_kernel, out_shape=(stream, stream, stream, half, half...  57.7 us

profile of v4, /device:TPU:32, one launch (start us, length us, event | category | flops | bytes accessed | tf_op | source)
XLA Modules:
  0.0 59.9 jit_solution(906167781968542687)
XLA Ops:
  0.6 0.0 copy-start
  0.6 0.7 %copy-done = f32[512,3]{0,1:T(4,128)S(1)} copy-done((f32[512,3]{0,1:T(4,128)S(1)}, f32[512,3]{0,1:T(4,128)}, u32[]{:S(2)}) %copy-start) | copy-done | bytes 6168
  1.3 57.7 %exchange.1 = (bf16[512,128]{1,0:T(8,128)(2,1)S(1)}, bf16[512,128]{1,0:T(8,128)(2,1)S(1)}, bf16[512,128]{1,0:T(8,128)(2,1)S(1)}, f32[8,4096]{1,0:T(8,128)S(1)}, ...) custom-call(bf16[512,128]{1,0:T(8,128)(2,1)} %q_hbm.1, bf16[512,128]{1,0:T(8,128)(2,1)} %k_hbm.1, bf16[512,128]{1,0:T(8,128)(2,1)} %v_hbm.1, ...), custom_call_target="tpu_custom_call" | custom-call | tf_op jit(solution)/shard_map/exchange/pallas_call | solution.py:401
  59.1 0.9 %write.1 = (bf16[512,128]{1,0:T(8,128)(2,1)}, bf16[512,128]{1,0:T(8,128)(2,1)}, bf16[512,128]{1,0:T(8,128)(2,1)}, f32[8,8192]{1,0:T(8,128)}, f32[3,512]{1,0:T(4,128)}) custom-call(bf16[512,128]{1,0:T(8,128)(2,1)S(1)} %get-tuple-element.16.qg, bf16[512,128]{1,0:T(8,128)(2,1)S(1)} %get-tuple-element.17.kg, bf16[512,128]{1,0:T(8,128)(2,1)S(1)} %get-tuple-element.18.vg, ...), custom_call_target="tpu_custom_call" | custom-call | tf_op jit(solution)/shard_map/write/pallas_call | solution.py:433
Async XLA Ops:
  0.6 0.7 %copy-start = (f32[512,3]{0,1:T(4,128)S(1)}, f32[512,3]{0,1:T(4,128)}, u32[]{:S(2)}) copy-start(f32[512,3]{0,1:T(4,128)} %param.12) | copy-start | bytes 18436
